TPU v7x, 32 devices: a whole 2x2x4 slice. The times are simulated.
32 devices in a mesh: ty: 8 (over z, y), tx: 4 (over x, core).
Axes of the slice: x: 2, y: 2, z: 4, core: 2. Of those that a mesh axis runs over, the one named last changes fastest.
Arguments:
- w_in: float32 [4, 8, 2, 256, 1024], P('tx', 'ty')
- w_out: float32 [4, 8, 2, 1024, 256], P('tx', 'ty')
- inputs: bfloat16 [4, 8, 9, 2048, 256], P('tx', 'ty')
- targets: bfloat16 [4, 8, 9, 2048, 256], P('tx', 'ty')
Outputs:
- output 1: float32 [4, 8, 2, 256, 1024], P('tx', 'ty')
- output 2: float32 [4, 8, 2, 1024, 256], P('tx', 'ty')
- output 3: float32 [4, 8, 2, 256, 1024], P('tx', 'ty')
- output 4: float32 [4, 8, 2, 1024, 256], P('tx', 'ty')
All inputs are finite; a program needn't handle non-finite values.
Results may differ from a plain program's by a relative error of at most 0.00727995.
Values are sent between devices in bfloat16 or wider.
A program may use at most 1 GiB of HBM per device.

v0:
```python
import jax
import jax.numpy as jnp
from jax import lax
from jax.sharding import PartitionSpec as P

EPS = 1e-6
LEARN_RATE = 0.125


def layer_step(hidden, mat_in, mat_out):
    hidden_f32 = hidden.astype(jnp.float32)
    inv_rms = lax.rsqrt(jnp.mean(hidden_f32 * hidden_f32, axis=-1, keepdims=True) + EPS)
    normed = (hidden_f32 * inv_rms).astype(jnp.bfloat16)
    pre_act = jnp.dot(normed, mat_in.astype(jnp.bfloat16), preferred_element_type=jnp.float32)
    gelu_out = jax.nn.gelu(pre_act).astype(jnp.bfloat16)
    mlp_out = jnp.dot(gelu_out, mat_out.astype(jnp.bfloat16), preferred_element_type=jnp.float32)
    return (hidden_f32 + mlp_out).astype(jnp.bfloat16)


def local_loss(w_in, w_out, batch_in, batch_tgt):
    hidden = batch_in
    for layer_idx in range(w_in.shape[0]):
        hidden = layer_step(hidden, w_in[layer_idx], w_out[layer_idx])
    resid_err = hidden.astype(jnp.float32) - batch_tgt.astype(jnp.float32)
    return jnp.mean(resid_err * resid_err)


local_grads = jax.grad(local_loss, argnums=(0, 1))


def neighbour_shift(values, axis_name, axis_size, offset):
    perm_pairs = [(source, (source + offset) % axis_size) for source in range(axis_size)]
    return lax.ppermute(values, axis_name, perm_pairs)


def solution(mesh):
    size_x = mesh.shape['tx']
    size_y = mesh.shape['ty']

    def gossip_mix(values):
        sent_copy = values.astype(jnp.bfloat16)
        from_xm = neighbour_shift(sent_copy, 'tx', size_x, 1)
        from_xp = neighbour_shift(sent_copy, 'tx', size_x, -1)
        from_ym = neighbour_shift(sent_copy, 'ty', size_y, 1)
        from_yp = neighbour_shift(sent_copy, 'ty', size_y, -1)
        summed = values + from_xm.astype(jnp.float32)
        summed = summed + from_xp.astype(jnp.float32)
        summed = summed + from_ym.astype(jnp.float32)
        summed = summed + from_yp.astype(jnp.float32)
        return summed / 5.0

    def device_fn(w_in, w_out, inputs, targets):
        p_in = w_in[0, 0]
        p_out = w_out[0, 0]
        batch_in = inputs[0, 0]
        batch_tgt = targets[0, 0]
        step_size = LEARN_RATE
        grad_in, grad_out = local_grads(p_in, p_out, batch_in[0], batch_tgt[0])
        y_in, y_out = grad_in, grad_out
        for step_idx in range(1, batch_in.shape[0]):
            p_in = gossip_mix(p_in) - step_size * y_in
            p_out = gossip_mix(p_out) - step_size * y_out
            mixed_yin = gossip_mix(y_in)
            mixed_yout = gossip_mix(y_out)
            new_gin, new_gout = local_grads(p_in, p_out, batch_in[step_idx], batch_tgt[step_idx])
            y_in = mixed_yin + new_gin - grad_in
            y_out = mixed_yout + new_gout - grad_out
            grad_in, grad_out = new_gin, new_gout
        return p_in[None, None], p_out[None, None], y_in[None, None], y_out[None, None]

    block_spec = P('tx', 'ty')
    return jax.shard_map(device_fn, mesh=mesh, in_specs=(block_spec, block_spec, block_spec, block_spec), out_specs=(block_spec, block_spec, block_spec, block_spec), check_vma=False)
```

profile of v0, /device:TPU:0, one launch (start us, length us, event | category | flops | bytes accessed | tf_op | source)
XLA Modules:
  0.0 1581.9 jit_solution(4443990940421381248)
XLA Ops:
  140.1 47.7 %collective-permute-done.14 = bf16[2,1024,256]{2,1,0:T(8,128)(2,1)S(1)} collective-permute-done((bf16[2,1024,256]{2,1,0:T(8,128)(2,1)}, bf16[2,1024,256]{2,1,0:T(8,128)(2,1)S(1)}, u32[]{:S(2)}, u32[]{:S(2)}) %collective-permute-start.14) | collective-permute-done | bytes 1048608 | tf_op jit(solution)/shard_map/ppermute | solution.py:33
  416.7 23.3 %collective-permute-done.18 = bf16[2,256,1024]{2,1,0:T(8,128)(2,1)} collective-permute-done((bf16[2,256,1024]{2,1,0:T(8,128)(2,1)}, bf16[2,256,1024]{2,1,0:T(8,128)(2,1)}, u32[]{:S(2)}, u32[]{:S(2)}) %collective-permute-start.18) | collective-permute-done | bytes 1048608 | tf_op jit(solution)/shard_map/ppermute | solution.py:33
  489.6 21.0 %collective-permute-done.47 = bf16[2,1024,256]{2,1,0:T(8,128)(2,1)S(1)} collective-permute-done((bf16[2,1024,256]{2,1,0:T(8,128)(2,1)}, bf16[2,1024,256]{2,1,0:T(8,128)(2,1)S(1)}, u32[]{:S(2)}, u32[]{:S(2)}) %collective-permute-start.47) | collective-permute-done | bytes 1048608 | tf_op jit(solution)/shard_map/ppermute | solution.py:33
  601.3 22.5 %collective-permute-done.34 = bf16[2,256,1024]{2,1,0:T(8,128)(2,1)} collective-permute-done((bf16[2,256,1024]{2,1,0:T(8,128)(2,1)}, bf16[2,256,1024]{2,1,0:T(8,128)(2,1)}, u32[]{:S(2)}, u32[]{:S(2)}) %collective-permute-start.34) | collective-permute-done | bytes 1048608 | tf_op jit(solution)/shard_map/ppermute | solution.py:33
  628.9 20.9 %collective-permute-done.35 = bf16[2,256,1024]{2,1,0:T(8,128)(2,1)S(1)} collective-permute-done((bf16[2,256,1024]{2,1,0:T(8,128)(2,1)}, bf16[2,256,1024]{2,1,0:T(8,128)(2,1)S(1)}, u32[]{:S(2)}, u32[]{:S(2)}) %collective-permute-start.35) | collective-permute-done | bytes 1048608 | tf_op jit(solution)/shard_map/ppermute | solution.py:33
  671.9 22.2 %collective-permute-done.63 = bf16[2,1024,256]{2,1,0:T(8,128)(2,1)S(1)} collective-permute-done((bf16[2,1024,256]{2,1,0:T(8,128)(2,1)S(1)}, bf16[2,1024,256]{2,1,0:T(8,128)(2,1)S(1)}, u32[]{:S(2)}, u32[]{:S(2)}) %collective-permute-start.63) | collective-permute-done | bytes 1048608 | tf_op jit(solution)/shard_map/ppermute | solution.py:33
  716.3 22.2 %collective-permute-done.59 = bf16[2,1024,256]{2,1,0:T(8,128)(2,1)S(1)} collective-permute-done((bf16[2,1024,256]{2,1,0:T(8,128)(2,1)S(1)}, bf16[2,1024,256]{2,1,0:T(8,128)(2,1)S(1)}, u32[]{:S(2)}, u32[]{:S(2)}) %collective-permute-start.59) | collective-permute-done | bytes 1048608 | tf_op jit(solution)/shard_map/ppermute | solution.py:33
  784.2 23.2 %collective-permute-done.50 = bf16[2,256,1024]{2,1,0:T(8,128)(2,1)} collective-permute-done((bf16[2,256,1024]{2,1,0:T(8,128)(2,1)}, bf16[2,256,1024]{2,1,0:T(8,128)(2,1)}, u32[]{:S(2)}, u32[]{:S(2)}) %collective-permute-start.50) | collective-permute-done | bytes 1048608 | tf_op jit(solution)/shard_map/ppermute | solution.py:33
  812.4 21.3 %collective-permute-done.51 = bf16[2,256,1024]{2,1,0:T(8,128)(2,1)S(1)} collective-permute-done((bf16[2,256,1024]{2,1,0:T(8,128)(2,1)}, bf16[2,256,1024]{2,1,0:T(8,128)(2,1)S(1)}, u32[]{:S(2)}, u32[]{:S(2)}) %collective-permute-start.51) | collective-permute-done | bytes 1048608 | tf_op jit(solution)/shard_map/ppermute | solution.py:33
  855.6 22.4 %collective-permute-done.79 = bf16[2,1024,256]{2,1,0:T(8,128)(2,1)S(1)} collective-permute-done((bf16[2,1024,256]{2,1,0:T(8,128)(2,1)S(1)}, bf16[2,1024,256]{2,1,0:T(8,128)(2,1)S(1)}, u32[]{:S(2)}, u32[]{:S(2)}) %collective-permute-start.79) | collective-permute-done | bytes 1048608 | tf_op jit(solution)/shard_map/ppermute | solution.py:33
  900.1 22.2 %collective-permute-done.75 = bf16[2,1024,256]{2,1,0:T(8,128)(2,1)S(1)} collective-permute-done((bf16[2,1024,256]{2,1,0:T(8,128)(2,1)S(1)}, bf16[2,1024,256]{2,1,0:T(8,128)(2,1)S(1)}, u32[]{:S(2)}, u32[]{:S(2)}) %collective-permute-start.75) | collective-permute-done | bytes 1048608 | tf_op jit(solution)/shard_map/ppermute | solution.py:33
  968.8 22.5 %collective-permute-done.66 = bf16[2,256,1024]{2,1,0:T(8,128)(2,1)} collective-permute-done((bf16[2,256,1024]{2,1,0:T(8,128)(2,1)}, bf16[2,256,1024]{2,1,0:T(8,128)(2,1)}, u32[]{:S(2)}, u32[]{:S(2)}) %collective-permute-start.66) | collective-permute-done | bytes 1048608 | tf_op jit(solution)/shard_map/ppermute | solution.py:33
  994.9 22.4 %collective-permute-done.67 = bf16[2,256,1024]{2,1,0:T(8,128)(2,1)S(1)} collective-permute-done((bf16[2,256,1024]{2,1,0:T(8,128)(2,1)}, bf16[2,256,1024]{2,1,0:T(8,128)(2,1)S(1)}, u32[]{:S(2)}, u32[]{:S(2)}) %collective-permute-start.67) | collective-permute-done | bytes 1048608 | tf_op jit(solution)/shard_map/ppermute | solution.py:33
  1037.9 23.7 %collective-permute-done.95 = bf16[2,1024,256]{2,1,0:T(8,128)(2,1)S(1)} collective-permute-done((bf16[2,1024,256]{2,1,0:T(8,128)(2,1)S(1)}, bf16[2,1024,256]{2,1,0:T(8,128)(2,1)S(1)}, u32[]{:S(2)}, u32[]{:S(2)}) %collective-permute-start.95) | collective-permute-done | bytes 1048608 | tf_op jit(solution)/shard_map/ppermute | solution.py:33
  1082.3 23.7 %collective-permute-done.91 = bf16[2,1024,256]{2,1,0:T(8,128)(2,1)S(1)} collective-permute-done((bf16[2,1024,256]{2,1,0:T(8,128)(2,1)S(1)}, bf16[2,1024,256]{2,1,0:T(8,128)(2,1)S(1)}, u32[]{:S(2)}, u32[]{:S(2)}) %collective-permute-start.91) | collective-permute-done | bytes 1048608 | tf_op jit(solution)/shard_map/ppermute | solution.py:33
  1151.8 23.2 %collective-permute-done.82 = bf16[2,256,1024]{2,1,0:T(8,128)(2,1)} collective-permute-done((bf16[2,256,1024]{2,1,0:T(8,128)(2,1)}, bf16[2,256,1024]{2,1,0:T(8,128)(2,1)}, u32[]{:S(2)}, u32[]{:S(2)}) %collective-permute-start.82) | collective-permute-done | bytes 1048608 | tf_op jit(solution)/shard_map/ppermute | solution.py:33
  1178.5 22.7 %collective-permute-done.83 = bf16[2,256,1024]{2,1,0:T(8,128)(2,1)S(1)} collective-permute-done((bf16[2,256,1024]{2,1,0:T(8,128)(2,1)}, bf16[2,256,1024]{2,1,0:T(8,128)(2,1)S(1)}, u32[]{:S(2)}, u32[]{:S(2)}) %collective-permute-start.83) | collective-permute-done | bytes 1048608 | tf_op jit(solution)/shard_map/ppermute | solution.py:33
  1221.7 23.8 %collective-permute-done.111 = bf16[2,1024,256]{2,1,0:T(8,128)(2,1)S(1)} collective-permute-done((bf16[2,1024,256]{2,1,0:T(8,128)(2,1)S(1)}, bf16[2,1024,256]{2,1,0:T(8,128)(2,1)S(1)}, u32[]{:S(2)}, u32[]{:S(2)}) %collective-permute-start.111) | collective-permute-done | bytes 1048608 | tf_op jit(solution)/shard_map/ppermute | solution.py:33
  1264.6 25.3 %collective-permute-done.107 = bf16[2,1024,256]{2,1,0:T(8,128)(2,1)S(1)} collective-permute-done((bf16[2,1024,256]{2,1,0:T(8,128)(2,1)S(1)}, bf16[2,1024,256]{2,1,0:T(8,128)(2,1)S(1)}, u32[]{:S(2)}, u32[]{:S(2)}) %collective-permute-start.107) | collective-permute-done | bytes 1048608 | tf_op jit(solution)/shard_map/ppermute | solution.py:33
  1332.1 44.6 %collective-permute-done.118 = bf16[2,1024,256]{2,1,0:T(8,128)(2,1)} collective-permute-done((bf16[2,1024,256]{2,1,0:T(8,128)(2,1)}, bf16[2,1024,256]{2,1,0:T(8,128)(2,1)}, u32[]{:S(2)}, u32[]{:S(2)}) %collective-permute-start.118) | collective-permute-done | bytes 1048608 | tf_op jit(solution)/shard_map/ppermute | solution.py:33
  1391.2 33.3 %collective-permute-done.98 = bf16[2,256,1024]{2,1,0:T(8,128)(2,1)S(1)} collective-permute-done((bf16[2,256,1024]{2,1,0:T(8,128)(2,1)S(1)}, bf16[2,256,1024]{2,1,0:T(8,128)(2,1)S(1)}, u32[]{:S(2)}, u32[]{:S(2)}) %collective-permute-start.98) | collective-permute-done | bytes 1048608 | tf_op jit(solution)/shard_map/ppermute | solution.py:33
  1425.3 23.5 %collective-permute-done.99 = bf16[2,256,1024]{2,1,0:T(8,128)(2,1)S(1)} collective-permute-done((bf16[2,256,1024]{2,1,0:T(8,128)(2,1)S(1)}, bf16[2,256,1024]{2,1,0:T(8,128)(2,1)S(1)}, u32[]{:S(2)}, u32[]{:S(2)}) %collective-permute-start.99) | collective-permute-done | bytes 1048608 | tf_op jit(solution)/shard_map/ppermute | solution.py:33
  1469.8 23.4 %collective-permute-done.115 = bf16[2,1024,256]{2,1,0:T(8,128)(2,1)S(1)} collective-permute-done((bf16[2,1024,256]{2,1,0:T(8,128)(2,1)S(1)}, bf16[2,1024,256]{2,1,0:T(8,128)(2,1)S(1)}, u32[]{:S(2)}, u32[]{:S(2)}) %collective-permute-start.115) | collective-permute-done | bytes 1048608 | tf_op jit(solution)/shard_map/ppermute | solution.py:33
  1542.7 32.5 %collective-permute-done.122 = bf16[2,256,1024]{2,1,0:T(8,128)(2,1)S(1)} collective-permute-done((bf16[2,256,1024]{2,1,0:T(8,128)(2,1)}, bf16[2,256,1024]{2,1,0:T(8,128)(2,1)S(1)}, u32[]{:S(2)}, u32[]{:S(2)}) %collective-permute-start.122) | collective-permute-done | bytes 1048608 | tf_op jit(solution)/shard_map/ppermute | solution.py:33
  (918 shorter events, 964.2 us)
Async XLA Ops:
  4.3 113.4 %collective-permute-start = (bf16[2,256,1024]{2,1,0:T(8,128)(2,1)}, bf16[2,256,1024]{2,1,0:T(8,128)(2,1)}, u32[]{:S(2)}, u32[]{:S(2)}) collective-permute-start(bf16[2,256,1024]{2,1,0:T(8,128)(2,1)} %get-tuple-element.77), channel_id=1, source_target_pairs={{0,1},{1,2},{2,3},{3,0},{4,5},{5,6},{6,7},{7,4},{8,9},{9,10},{10,1... | collective-permute-start | bytes 3145736 | tf_op jit(solution)/shard_map/ppermute | solution.py:33
  4.8 114.7 %collective-permute-start.1 = (bf16[2,256,1024]{2,1,0:T(8,128)(2,1)}, bf16[2,256,1024]{2,1,0:T(8,128)(2,1)}, u32[]{:S(2)}, u32[]{:S(2)}) collective-permute-start(bf16[2,256,1024]{2,1,0:T(8,128)(2,1)} %get-tuple-element.77), channel_id=1, source_target_pairs={{0,3},{1,0},{2,1},{3,2},{4,7},{5,4},{6,5},{7,6},{8,11},{9,8},{10,9... | collective-permute-start | bytes 3145736 | tf_op jit(solution)/shard_map/ppermute | solution.py:33
  6.8 112.8 %collective-permute-start.2 = (bf16[2,256,1024]{2,1,0:T(8,128)(2,1)}, bf16[2,256,1024]{2,1,0:T(8,128)(2,1)}, u32[]{:S(2)}, u32[]{:S(2)}) collective-permute-start(bf16[2,256,1024]{2,1,0:T(8,128)(2,1)} %get-tuple-element.77), channel_id=1, source_target_pairs={{0,4},{4,8},{8,12},{12,16},{16,20},{20,24},{24,28},{28,0},{1,5},{5... | collective-permute-start | bytes 3145736 | tf_op jit(solution)/shard_map/ppermute | solution.py:33
  9.1 115.1 %collective-permute-start.3 = (bf16[2,256,1024]{2,1,0:T(8,128)(2,1)}, bf16[2,256,1024]{2,1,0:T(8,128)(2,1)}, u32[]{:S(2)}, u32[]{:S(2)}) collective-permute-start(bf16[2,256,1024]{2,1,0:T(8,128)(2,1)} %get-tuple-element.77), channel_id=1, source_target_pairs={{0,28},{4,0},{8,4},{12,8},{16,12},{20,16},{24,20},{28,24},{1,29},{... | collective-permute-start | bytes 3145736 | tf_op jit(solution)/shard_map/ppermute | solution.py:33
  13.7 121.7 %collective-permute-start.12 = (bf16[2,1024,256]{2,1,0:T(8,128)(2,1)}, bf16[2,1024,256]{2,1,0:T(8,128)(2,1)}, u32[]{:S(2)}, u32[]{:S(2)}) collective-permute-start(bf16[2,1024,256]{2,1,0:T(8,128)(2,1)} %get-tuple-element.75), channel_id=1, source_target_pairs={{0,1},{1,2},{2,3},{3,0},{4,5},{5,6},{6,7},{7,4},{8,9},{9,10},{10,1... | collective-permute-start | bytes 3145736 | tf_op jit(solution)/shard_map/ppermute | solution.py:33
  119.5 70.6 %collective-permute-start.15 = (bf16[2,1024,256]{2,1,0:T(8,128)(2,1)}, bf16[2,1024,256]{2,1,0:T(8,128)(2,1)S(1)}, u32[]{:S(2)}, u32[]{:S(2)}) collective-permute-start(bf16[2,1024,256]{2,1,0:T(8,128)(2,1)} %get-tuple-element.75), channel_id=1, source_target_pairs={{0,28},{4,0},{8,4},{12,8},{16,12},{20,16},{24,20},{28,24},{1,29},{... | collective-permute-start | bytes 3145736 | tf_op jit(solution)/shard_map/ppermute | solution.py:33
  129.1 84.0 %collective-permute-start.10 = (bf16[2,256,1024]{2,1,0:T(8,128)(2,1)}, bf16[2,256,1024]{2,1,0:T(8,128)(2,1)}, u32[]{:S(2)}, u32[]{:S(2)}) collective-permute-start(bf16[2,256,1024]{2,1,0:T(8,128)(2,1)} %get-tuple-element.80), channel_id=1, source_target_pairs={{0,4},{4,8},{8,12},{12,16},{16,20},{20,24},{24,28},{28,0},{1,5},{5... | collective-permute-start | bytes 3145736 | tf_op jit(solution)/shard_map/ppermute | solution.py:33
  135.4 99.1 %collective-permute-start.11 = (bf16[2,256,1024]{2,1,0:T(8,128)(2,1)}, bf16[2,256,1024]{2,1,0:T(8,128)(2,1)}, u32[]{:S(2)}, u32[]{:S(2)}) collective-permute-start(bf16[2,256,1024]{2,1,0:T(8,128)(2,1)} %get-tuple-element.80), channel_id=1, source_target_pairs={{0,28},{4,0},{8,4},{12,8},{16,12},{20,16},{24,20},{28,24},{1,29},{... | collective-permute-start | bytes 3145736 | tf_op jit(solution)/shard_map/ppermute | solution.py:33
  140.1 106.3 %collective-permute-start.4 = (bf16[2,256,1024]{2,1,0:T(8,128)(2,1)}, bf16[2,256,1024]{2,1,0:T(8,128)(2,1)}, u32[]{:S(2)}, u32[]{:S(2)}) collective-permute-start(bf16[2,256,1024]{2,1,0:T(8,128)(2,1)} %get-tuple-element.55), channel_id=1, source_target_pairs={{0,1},{1,2},{2,3},{3,0},{4,5},{5,6},{6,7},{7,4},{8,9},{9,10},{10,1... | collective-permute-start | bytes 3145736 | tf_op jit(solution)/shard_map/ppermute | solution.py:33
  440.0 70.5 %collective-permute-start.47 = (bf16[2,1024,256]{2,1,0:T(8,128)(2,1)}, bf16[2,1024,256]{2,1,0:T(8,128)(2,1)S(1)}, u32[]{:S(2)}, u32[]{:S(2)}) collective-permute-start(bf16[2,1024,256]{2,1,0:T(8,128)(2,1)} %get-tuple-element.43), channel_id=1, source_target_pairs={{0,28},{4,0},{8,4},{12,8},{16,12},{20,16},{24,20},{28,24},{1,29},{... | collective-permute-start | bytes 3145736 | tf_op jit(solution)/shard_map/ppermute | solution.py:33
  484.8 70.1 %collective-permute-start.43 = (bf16[2,1024,256]{2,1,0:T(8,128)(2,1)S(1)}, bf16[2,1024,256]{2,1,0:T(8,128)(2,1)S(1)}, u32[]{:S(2)}, u32[]{:S(2)}) collective-permute-start(bf16[2,1024,256]{2,1,0:T(8,128)(2,1)S(1)} %copy-done.174), channel_id=1, source_target_pairs={{0,28},{4,0},{8,4},{12,8},{16,12},{20,16},{24,20},{28,24},{1,29},{... | collective-permute-start | bytes 3145736 | tf_op jit(solution)/shard_map/ppermute | solution.py:33
  623.8 70.4 %collective-permute-start.63 = (bf16[2,1024,256]{2,1,0:T(8,128)(2,1)S(1)}, bf16[2,1024,256]{2,1,0:T(8,128)(2,1)S(1)}, u32[]{:S(2)}, u32[]{:S(2)}) collective-permute-start(bf16[2,1024,256]{2,1,0:T(8,128)(2,1)S(1)} %copy-done.175), channel_id=1, source_target_pairs={{0,28},{4,0},{8,4},{12,8},{16,12},{20,16},{24,20},{28,24},{1,29},{... | collective-permute-start | bytes 3145736 | tf_op jit(solution)/shard_map/ppermute | solution.py:33
  668.6 69.9 %collective-permute-start.59 = (bf16[2,1024,256]{2,1,0:T(8,128)(2,1)S(1)}, bf16[2,1024,256]{2,1,0:T(8,128)(2,1)S(1)}, u32[]{:S(2)}, u32[]{:S(2)}) collective-permute-start(bf16[2,1024,256]{2,1,0:T(8,128)(2,1)S(1)} %copy-done.177), channel_id=1, source_target_pairs={{0,28},{4,0},{8,4},{12,8},{16,12},{20,16},{24,20},{28,24},{1,29},{... | collective-permute-start | bytes 3145736 | tf_op jit(solution)/shard_map/ppermute | solution.py:33
  807.5 70.5 %collective-permute-start.79 = (bf16[2,1024,256]{2,1,0:T(8,128)(2,1)S(1)}, bf16[2,1024,256]{2,1,0:T(8,128)(2,1)S(1)}, u32[]{:S(2)}, u32[]{:S(2)}) collective-permute-start(bf16[2,1024,256]{2,1,0:T(8,128)(2,1)S(1)} %copy-done.178), channel_id=1, source_target_pairs={{0,28},{4,0},{8,4},{12,8},{16,12},{20,16},{24,20},{28,24},{1,29},{... | collective-permute-start | bytes 3145736 | tf_op jit(solution)/shard_map/ppermute | solution.py:33
  852.3 70.1 %collective-permute-start.75 = (bf16[2,1024,256]{2,1,0:T(8,128)(2,1)S(1)}, bf16[2,1024,256]{2,1,0:T(8,128)(2,1)S(1)}, u32[]{:S(2)}, u32[]{:S(2)}) collective-permute-start(bf16[2,1024,256]{2,1,0:T(8,128)(2,1)S(1)} %copy-done.180), channel_id=1, source_target_pairs={{0,28},{4,0},{8,4},{12,8},{16,12},{20,16},{24,20},{28,24},{1,29},{... | collective-permute-start | bytes 3145736 | tf_op jit(solution)/shard_map/ppermute | solution.py:33
  991.2 70.4 %collective-permute-start.95 = (bf16[2,1024,256]{2,1,0:T(8,128)(2,1)S(1)}, bf16[2,1024,256]{2,1,0:T(8,128)(2,1)S(1)}, u32[]{:S(2)}, u32[]{:S(2)}) collective-permute-start(bf16[2,1024,256]{2,1,0:T(8,128)(2,1)S(1)} %copy-done.181), channel_id=1, source_target_pairs={{0,28},{4,0},{8,4},{12,8},{16,12},{20,16},{24,20},{28,24},{1,29},{... | collective-permute-start | bytes 3145736 | tf_op jit(solution)/shard_map/ppermute | solution.py:33
  1036.0 69.9 %collective-permute-start.91 = (bf16[2,1024,256]{2,1,0:T(8,128)(2,1)S(1)}, bf16[2,1024,256]{2,1,0:T(8,128)(2,1)S(1)}, u32[]{:S(2)}, u32[]{:S(2)}) collective-permute-start(bf16[2,1024,256]{2,1,0:T(8,128)(2,1)S(1)} %copy-done.183), channel_id=1, source_target_pairs={{0,28},{4,0},{8,4},{12,8},{16,12},{20,16},{24,20},{28,24},{1,29},{... | collective-permute-start | bytes 3145736 | tf_op jit(solution)/shard_map/ppermute | solution.py:33
  1175.0 70.5 %collective-permute-start.111 = (bf16[2,1024,256]{2,1,0:T(8,128)(2,1)S(1)}, bf16[2,1024,256]{2,1,0:T(8,128)(2,1)S(1)}, u32[]{:S(2)}, u32[]{:S(2)}) collective-permute-start(bf16[2,1024,256]{2,1,0:T(8,128)(2,1)S(1)} %copy-done.184), channel_id=1, source_target_pairs={{0,28},{4,0},{8,4},{12,8},{16,12},{20,16},{24,20},{28,24},{1,29},{... | collective-permute-start | bytes 3145736 | tf_op jit(solution)/shard_map/ppermute | solution.py:33
  1219.8 70.1 %collective-permute-start.107 = (bf16[2,1024,256]{2,1,0:T(8,128)(2,1)S(1)}, bf16[2,1024,256]{2,1,0:T(8,128)(2,1)S(1)}, u32[]{:S(2)}, u32[]{:S(2)}) collective-permute-start(bf16[2,1024,256]{2,1,0:T(8,128)(2,1)S(1)} %copy-done.186), channel_id=1, source_target_pairs={{0,28},{4,0},{8,4},{12,8},{16,12},{20,16},{24,20},{28,24},{1,29},{... | collective-permute-start | bytes 3145736 | tf_op jit(solution)/shard_map/ppermute | solution.py:33
  1254.3 75.9 %collective-permute-start.102 = (bf16[2,256,1024]{2,1,0:T(8,128)(2,1)}, bf16[2,256,1024]{2,1,0:T(8,128)(2,1)}, u32[]{:S(2)}, u32[]{:S(2)}) collective-permute-start(bf16[2,256,1024]{2,1,0:T(8,128)(2,1)} %convert_element_type.1744), channel_id=1, source_target_pairs={{0,4},{4,8},{8,12},{12,16},{16,20},{20,24},{24,28},{28,0},{1,5},{5... | collective-permute-start | bytes 3145736 | tf_op jit(solution)/shard_map/ppermute | solution.py:33
  1389.3 71.5 %collective-permute-start.113 = (bf16[2,1024,256]{2,1,0:T(8,128)(2,1)S(1)}, bf16[2,1024,256]{2,1,0:T(8,128)(2,1)S(1)}, u32[]{:S(2)}, u32[]{:S(2)}) collective-permute-start(bf16[2,1024,256]{2,1,0:T(8,128)(2,1)S(1)} %copy-done.188), channel_id=1, source_target_pairs={{0,3},{1,0},{2,1},{3,2},{4,7},{5,4},{6,5},{7,6},{8,11},{9,8},{10,9... | collective-permute-start | bytes 3145736 | tf_op jit(solution)/shard_map/ppermute | solution.py:33
  1391.1 78.3 %collective-permute-start.114 = (bf16[2,1024,256]{2,1,0:T(8,128)(2,1)S(1)}, bf16[2,1024,256]{2,1,0:T(8,128)(2,1)S(1)}, u32[]{:S(2)}, u32[]{:S(2)}) collective-permute-start(bf16[2,1024,256]{2,1,0:T(8,128)(2,1)S(1)} %copy-done.188), channel_id=1, source_target_pairs={{0,4},{4,8},{8,12},{12,16},{16,20},{20,24},{24,28},{28,0},{1,5},{5... | collective-permute-start | bytes 3145736 | tf_op jit(solution)/shard_map/ppermute | solution.py:33
  1448.8 79.8 %collective-permute-start.124 = (bf16[2,1024,256]{2,1,0:T(8,128)(2,1)}, bf16[2,1024,256]{2,1,0:T(8,128)(2,1)}, u32[]{:S(2)}, u32[]{:S(2)}) collective-permute-start(bf16[2,1024,256]{2,1,0:T(8,128)(2,1)} %get-tuple-element.4), channel_id=1, source_target_pairs={{0,1},{1,2},{2,3},{3,0},{4,5},{5,6},{6,7},{7,4},{8,9},{9,10},{10,1... | collective-permute-start | bytes 3145736 | tf_op jit(solution)/shard_map/ppermute | solution.py:33
  1459.1 71.3 %collective-permute-start.125 = (bf16[2,1024,256]{2,1,0:T(8,128)(2,1)}, bf16[2,1024,256]{2,1,0:T(8,128)(2,1)S(1)}, u32[]{:S(2)}, u32[]{:S(2)}) collective-permute-start(bf16[2,1024,256]{2,1,0:T(8,128)(2,1)} %get-tuple-element.4), channel_id=1, source_target_pairs={{0,3},{1,0},{2,1},{3,2},{4,7},{5,4},{6,5},{7,6},{8,11},{9,8},{10,9... | collective-permute-start | bytes 3145736 | tf_op jit(solution)/shard_map/ppermute | solution.py:33
  (352 other events, 12960.2 us)
where the time goes:
time: 1590 us; the launch traced here: 1580 us
  waiting for transfers between devices  858 us (54%)
  matrix products  360 us (23%)
  starting transfers between devices  173 us (11%)
  other arithmetic  128 us (8%)
  local copies, waits for them, and re-layouts  59.2 us (4%)
    ppermute x128, waiting for transfers between devices, neighbour_shift(): return lax.ppermute(values, axis_name, perm_pairs)  858 us
    dot_general x45, matrix products, layer_step(): jnp.dot(normed, mat_in.astype(jnp.bfloat16), preferred_element_type=jnp.f...  226 us
    ppermute x128, starting transfers between devices, neighbour_shift(): return lax.ppermute(values, axis_name, perm_pairs)  173 us
    dot_general x45, matrix products, layer_step(): jnp.dot(gelu_out, mat_out.astype(jnp.bfloat16), preferred_element_type=jn...  134 us
    convert_element_type x23, other arithmetic, gossip_mix(): sent_copy = values.astype(jnp.bfloat16)  68.6 us
    unnamed x514, local copies, waits for them, and re-layouts  49.7 us
  transfers between devices with their start and end apart: 128, of which 50 were waited for; matrix products, arithmetic and copies ran while one was open for 33% of the time, Pallas kernels for 0%

commit v1 on v0

v1 whole, which is shorter than its diff:
```python
import functools

import jax
import jax.numpy as jnp
from jax import lax
from jax.experimental import pallas as pl
from jax.experimental.pallas import tpu as pltpu
from jax.sharding import PartitionSpec as P

EPS = 1e-6
LEARN_RATE = 0.125
UNITS = 8
BLOCKS = 8
GELU_C0 = 0.7978845608028654
GELU_C1 = 0.044715 * GELU_C0
F32 = jnp.float32
BF16 = jnp.bfloat16
MESH = pl.DeviceIdType.MESH


def dot(lhs, rhs, lhs_dim, rhs_dim):
    return lax.dot_general(lhs, rhs, (((lhs_dim,), (rhs_dim,)), ((), ())), preferred_element_type=F32)


def kernel(dims, win_hbm, wout_hbm, x_hbm, tgt_hbm, pin_hbm, pout_hbm, yin_hbm, yout_hbm,
           p_in, p_out, y_in, y_out, acc_in, acc_out, old_in, old_out,
           send_in, send_out, recv_in, recv_out, x_v, tgt_v, gp, act, unit_in, tmp, dz,
           recv_sem, send_sem, load_sem, store_sem):
    n_x, n_y, layers, d, ff, steps, rows = dims
    rb_rows = rows // BLOCKS
    ix, iy = lax.axis_index('tx'), lax.axis_index('ty')
    px, py = ix % 2, iy % 2
    partner = ix + 1 - 2 * px
    opposite = n_x - 1 - ix
    y_partner = iy + 1 - 2 * py
    relay_to = (iy + 2 * (1 - 2 * py) + n_y) % n_y
    relay_from = (iy - 2 * (1 - 2 * py) + n_y) % n_y
    to_partner = {'tx': partner, 'ty': iy}
    to_opposite = {'tx': opposite, 'ty': iy}
    to_y = {'tx': ix, 'ty': y_partner}
    to_z = {'tx': ix, 'ty': relay_to}
    y_dir = 3 - py
    z_dir = 2 + py

    barrier = pltpu.get_barrier_semaphore()
    for peer in (to_partner, to_opposite, to_y, to_z, {'tx': ix, 'ty': relay_from}):
        pl.semaphore_signal(barrier, inc=1, device_id=peer, device_id_type=MESH)

    piece = ((layers * d) // UNITS, (layers * ff) // UNITS)
    sends = (send_in, send_out)
    recvs = (recv_in, recv_out)

    def span(side, unit):
        return pl.ds(pl.multiple_of(unit * piece[side], piece[side]), piece[side])

    def direct(side, kind, unit, slot, dest):
        peer, where = ((to_partner, px), (to_opposite, 1 - px), (to_y, 2 + py))[dest]
        at = span(side, unit)
        return pltpu.make_async_remote_copy(
            src_ref=sends[side].at[kind, at],
            dst_ref=recvs[side].at[slot, kind, where, at],
            send_sem=send_sem.at[side, kind, unit, dest],
            recv_sem=recv_sem.at[side, slot, kind, unit, where],
            device_id=peer, device_id_type=MESH)

    def relay(side, kind, unit, slot):
        at = span(side, unit)
        return pltpu.make_async_remote_copy(
            src_ref=recvs[side].at[slot, kind, y_dir, at],
            dst_ref=recvs[side].at[slot, kind, z_dir, at],
            send_sem=send_sem.at[side, kind, unit, 3],
            recv_sem=recv_sem.at[side, slot, kind, unit, z_dir],
            device_id=to_z, device_id_type=MESH)

    def arrival(side, kind, unit, slot, where):
        at = span(side, unit)
        return pltpu.make_async_remote_copy(
            src_ref=sends[side].at[kind, at],
            dst_ref=recvs[side].at[slot, kind, where, at],
            send_sem=send_sem.at[side, kind, unit, 0],
            recv_sem=recv_sem.at[side, slot, kind, unit, where],
            device_id=to_partner, device_id_type=MESH)

    def send_piece(kind, unit, slot):
        for side in (0, 1):
            for dest in (2, 1, 0):
                direct(side, kind, unit, slot, dest).start()

    def forward(side, kind, unit, slot):
        arrival(side, kind, unit, slot, y_dir).wait_recv()
        relay(side, kind, unit, slot).start()

    def settle(kind, unit, slot):
        for side in (0, 1):
            for where in (0, 1, z_dir):
                arrival(side, kind, unit, slot, where).wait_recv()
            for dest in (0, 1, 2):
                direct(side, kind, unit, slot, dest).wait_send()
            relay(side, kind, unit, slot).wait_send()

    def batch_copies(step):
        return (pltpu.make_async_copy(x_hbm.at[step], x_v, load_sem.at[0]),
                pltpu.make_async_copy(tgt_hbm.at[step], tgt_v, load_sem.at[1]))

    weight_copies = (pltpu.make_async_copy(win_hbm, p_in, load_sem.at[2]),
                     pltpu.make_async_copy(wout_hbm, p_out, load_sem.at[3]))
    for copy in weight_copies + batch_copies(0):
        copy.start()
    for copy in weight_copies:
        copy.wait()

    def first_cast(unit, _):
        for side, weights in ((0, p_in), (1, p_out)):
            at = span(side, unit)
            sends[side][0, at] = weights[at].astype(BF16)
        return 0

    lax.fori_loop(0, UNITS, first_cast, 0)
    pl.semaphore_wait(barrier, 5)

    def first_send(unit, _):
        send_piece(0, unit, 0)
        return 0

    lax.fori_loop(0, UNITS, first_send, 0)

    def forward_layer(layer, hidden):
        w_in = send_in[0, layer * d:(layer + 1) * d]
        w_out = send_out[0, layer * ff:(layer + 1) * ff]
        inv_rms = lax.rsqrt(jnp.mean(hidden * hidden, axis=-1, keepdims=True) + EPS)
        normed = (hidden * inv_rms).astype(BF16)
        unit_in[layer] = normed
        gp[layer] = dot(normed, w_in, 1, 0)

        def activate(i, _):
            at = pl.ds(pl.multiple_of(i * 16, 16), 16)
            z = gp[layer, at]
            z2 = z * z
            tanh = jnp.tanh(z * (GELU_C0 + GELU_C1 * z2))
            cdf = 0.5 + 0.5 * tanh
            act[layer, at] = (z * cdf).astype(BF16)
            gp[layer, at] = cdf + (0.5 * z * (1.0 - tanh * tanh)) * (GELU_C0 + (3.0 * GELU_C1) * z2)
            return 0

        lax.fori_loop(0, rb_rows // 16, activate, 0)
        out = dot(act[layer], w_out, 1, 0)
        return (hidden + out).astype(BF16).astype(F32), inv_rms

    def backward_layer(layer, grad_b, hidden, inv_rms):
        w_in = send_in[0, layer * d:(layer + 1) * d]
        w_out = send_out[0, layer * ff:(layer + 1) * ff]
        tmp[...] = dot(grad_b, w_out, 1, 1)

        def chain(i, _):
            at = pl.ds(pl.multiple_of(i * 16, 16), 16)
            dz[at] = (tmp[at].astype(BF16).astype(F32) * gp[layer, at]).astype(BF16)
            return 0

        lax.fori_loop(0, rb_rows // 16, chain, 0)
        acc_out[layer * ff:(layer + 1) * ff] += dot(act[layer], grad_b, 0, 0)
        acc_in[layer * d:(layer + 1) * d] += dot(unit_in[layer], dz[...], 0, 0)
        if layer == 0:
            return None
        du = dot(dz[...], w_in, 1, 1).astype(BF16).astype(F32)
        proj = jnp.sum(du * hidden, axis=-1, keepdims=True) * (1.0 / d)
        grad = grad_b.astype(F32) + (du * inv_rms - hidden * (proj * (inv_rms * inv_rms * inv_rms)))
        return grad.astype(BF16)

    def phase(step, _):
        slot = step % 2
        for copy in batch_copies(step):
            copy.wait()
        acc_in[...] = jnp.zeros_like(acc_in)
        acc_out[...] = jnp.zeros_like(acc_out)
        edge = jnp.logical_or(step == 0, step == steps)

        def block(rb, _):
            kind = jnp.where(step == 0, 0, jnp.where(step == steps, 1, rb % 2))
            unit = jnp.where(edge, rb, rb // 2)
            at = pl.ds(pl.multiple_of(rb * rb_rows, rb_rows), rb_rows)
            hidden = [x_v[at].astype(F32)]
            scales = []
            for layer in range(layers):
                nxt, inv_rms = forward_layer(layer, hidden[-1])
                hidden.append(nxt)
                scales.append(inv_rms)
            forward(0, kind, unit, slot)
            grad = ((hidden[-1] - tgt_v[at].astype(F32)) * (2.0 / (rows * d))).astype(BF16)
            for layer in reversed(range(layers)):
                grad = backward_layer(layer, grad, hidden[layer], scales[layer])
            forward(1, kind, unit, slot)
            return 0

        lax.fori_loop(0, BLOCKS, block, 0)

        @pl.when(step < steps)
        def _():
            for copy in batch_copies(step + 1):
                copy.start()

        def update(unit, first, last):
            for side, sub, p, y, acc, old in ((0, 16, p_in, y_in, acc_in, old_in),
                                              (1, 64, p_out, y_out, acc_out, old_out)):
                def piece_step(s, _, side=side, sub=sub, p=p, y=y, acc=acc, old=old):
                    at = pl.ds(pl.multiple_of(unit * piece[side] + s * sub, sub), sub)

                    def mix(total, kind):
                        for where in range(4):
                            total = total + recvs[side][slot, kind, where, at].astype(F32)
                        return total / 5.0

                    g_b = acc[at].astype(BF16)
                    g = g_b.astype(F32)
                    if first:
                        tracker = g
                    else:
                        tracker = (mix(y[at], 1) + g) - old[at].astype(F32)
                    y[at] = tracker
                    if not last:
                        old[at] = g_b
                        weights = mix(p[at], 0) - LEARN_RATE * tracker
                        p[at] = weights
                        sends[side][0, at] = weights.astype(BF16)
                        sends[side][1, at] = tracker.astype(BF16)
                    return 0

                lax.fori_loop(0, piece[side] // sub, piece_step, 0)

        def unit_step(unit, _):
            @pl.when(step < steps)
            def _():
                settle(0, unit, slot)

            @pl.when(step > 0)
            def _():
                settle(1, unit, slot)

            @pl.when(step == 0)
            def _():
                update(unit, True, False)

            @pl.when(jnp.logical_not(edge))
            def _():
                update(unit, False, False)

            @pl.when(step == steps)
            def _():
                update(unit, False, True)

            @pl.when(step < steps - 1)
            def _():
                send_piece(0, unit, 1 - slot)

            @pl.when(step < steps)
            def _():
                send_piece(1, unit, 1 - slot)

            @pl.when(jnp.logical_and(jnp.logical_not(edge), unit < UNITS // 2))
            def _():
                for kind in (0, 1):
                    for side in (0, 1):
                        forward(side, kind, unit + UNITS // 2, slot)

            return 0

        lax.fori_loop(0, UNITS, unit_step, 0)
        return 0

    lax.fori_loop(0, steps + 1, phase, 0)
    stores = [pltpu.make_async_copy(src, dst, store_sem.at[k]) for k, (src, dst) in enumerate(
        ((p_in, pin_hbm), (p_out, pout_hbm), (y_in, yin_hbm), (y_out, yout_hbm)))]
    for copy in stores:
        copy.start()
    for copy in stores:
        copy.wait()


def solution(mesh):
    n_x, n_y = mesh.shape['tx'], mesh.shape['ty']

    def device_fn(w_in, w_out, inputs, targets):
        layers, d, ff = w_in.shape[2:]
        batches, rows = inputs.shape[2:4]
        dims = (n_x, n_y, layers, d, ff, batches - 1, rows)
        s_in, s_out = (layers * d, ff), (layers * ff, d)
        rb_rows = rows // BLOCKS
        vmem = pltpu.VMEM
        outs = pl.pallas_call(
            functools.partial(kernel, dims),
            out_shape=[jax.ShapeDtypeStruct(s, F32) for s in (s_in, s_out, s_in, s_out)],
            in_specs=[pl.BlockSpec(memory_space=pl.ANY)] * 4,
            out_specs=[pl.BlockSpec(memory_space=pl.ANY)] * 4,
            scratch_shapes=[
                vmem(s_in, F32), vmem(s_out, F32), vmem(s_in, F32), vmem(s_out, F32),
                vmem(s_in, F32), vmem(s_out, F32), vmem(s_in, BF16), vmem(s_out, BF16),
                vmem((2,) + s_in, BF16), vmem((2,) + s_out, BF16),
                vmem((2, 2, 4) + s_in, BF16), vmem((2, 2, 4) + s_out, BF16),
                vmem((rows, d), BF16), vmem((rows, d), BF16),
                vmem((layers, rb_rows, ff), F32), vmem((layers, rb_rows, ff), BF16),
                vmem((layers, rb_rows, d), BF16), vmem((rb_rows, ff), F32), vmem((rb_rows, ff), BF16),
                pltpu.SemaphoreType.DMA((2, 2, 2, UNITS, 4)),
                pltpu.SemaphoreType.DMA((2, 2, UNITS, 4)),
                pltpu.SemaphoreType.DMA((4,)),
                pltpu.SemaphoreType.DMA((4,)),
            ],
            compiler_params=pltpu.CompilerParams(
                collective_id=0, has_side_effects=True, vmem_limit_bytes=67043328),
        )(w_in.reshape(s_in), w_out.reshape(s_out), inputs[0, 0], targets[0, 0])
        return tuple(o.reshape(w.shape) for o, w in zip(outs, (w_in, w_out, w_in, w_out)))

    block_spec = P('tx', 'ty')
    return jax.shard_map(device_fn, mesh=mesh, in_specs=(block_spec,) * 4, out_specs=(block_spec,) * 4, check_vma=False)
```

time: 1590 us -> 794 us (0.50)
  waiting for transfers between devices: 858 us -> 0 us
  Pallas kernels: 0 us -> 784 us
  matrix products: 360 us -> 0 us
  starting transfers between devices: 173 us -> 0 us
  other arithmetic: 128 us -> 0 us
  local copies, waits for them, and re-layouts: 59.2 us -> 9.32 us
    ppermute x128 -> x0, waiting for transfers between devices: 858 us -> none  [neighbour_shift(): return lax.ppermute(values, axis_name, perm_pairs)]
    pallas_call x0 -> x1, Pallas kernels: none -> 784 us  [device_fn(): pl.pallas_call(functools.partial(kernel, dims), out_shape=[jax.ShapeDtype...]
    dot_general x90 -> x0, matrix products: 360 us -> none  [the longest x45 226 us: layer_step(): jnp.dot(normed, mat_in.astype(jnp.bfloat16), preferred_element_type=jnp.f...]
    ppermute x128 -> x0, starting transfers between devices: 173 us -> none  [neighbour_shift(): return lax.ppermute(values, axis_name, perm_pairs)]
    convert_element_type x32 -> x0, other arithmetic: 82.1 us -> none  [the longest x23 68.6 us: gossip_mix(): sent_copy = values.astype(jnp.bfloat16)]
    unnamed x514 -> x10, local copies, waits for them, and re-layouts: 49.7 us -> 9.32 us
    another operation x9 -> x0, other arithmetic: 24 us -> none
  transfers between devices with their start and end apart: 128 -> 0, of which waited for: 50 -> 0; matrix products, arithmetic and copies ran while one was open for 33% -> 0% of each run, Pallas kernels for 0% -> 0%
where the time goes in v1:
time: 794 us
  Pallas kernels  784 us (99%)
  local copies, waits for them, and re-layouts  9.32 us (1%)
    pallas_call x1, Pallas kernels, device_fn(): pl.pallas_call(functools.partial(kernel, dims), out_shape=[jax.ShapeDtype...  784 us

profile of v1, /device:TPU:0, one launch (start us, length us, event | category | flops | bytes accessed | tf_op | source)
XLA Modules:
  0.0 794.2 jit_solution(11134340313155985988)
XLA Ops:
  0.6 784.2 %shard_map.75 = (f32[512,1024]{1,0:T(8,128)}, f32[2048,256]{1,0:T(8,128)}, f32[512,1024]{1,0:T(8,128)}, f32[2048,256]{1,0:T(8,128)}) custom-call(f32[512,1024]{1,0:T(8,128)} %bitcast.14, f32[2048,256]{1,0:T(8,128)} %bitcast.15, bf16[9,2048,256]{2,1,0:T(8,128)(2,1)} %bitcast.8, bf16[9,2048,256]{2,1,0:T(8,128)(2,1)} %bitcast.9), custom_call_target="tpu_custom_call" | custom-call | tf_op jit(solution)/shard_map/pallas_call | solution.py:288
  784.9 0.0 copy-start.2
  784.9 3.3 copy.12
  788.2 0.0 copy-done.2
  788.2 0.0 copy-start.1
  788.2 1.3 copy.13
  789.5 1.0 copy-done.1
  790.5 0.0 copy-start
  790.5 1.3 copy.14
  791.8 1.0 copy-done
  792.9 1.3 copy.15
Async XLA Ops:
  784.9 3.3 copy-start.2
  788.2 2.3 copy-start.1
  790.5 2.3 copy-start

commit v2 on v1

--- a/solution.py
+++ b/solution.py
@@ -9,6 +9,7 @@
 
 EPS = 1e-6
 LEARN_RATE = 0.125
+VMEM_LIMIT = 54 * 1024 * 1024
 UNITS = 8
 BLOCKS = 8
 GELU_C0 = 0.7978845608028654
@@ -22,10 +23,9 @@
     return lax.dot_general(lhs, rhs, (((lhs_dim,), (rhs_dim,)), ((), ())), preferred_element_type=F32)
 
 
-def kernel(dims, win_hbm, wout_hbm, x_hbm, tgt_hbm, pin_hbm, pout_hbm, yin_hbm, yout_hbm,
-           p_in, p_out, y_in, y_out, acc_in, acc_out, old_in, old_out,
+def kernel(dims, win_hbm, wout_hbm, x_hbm, tgt_hbm, p_in, p_out, y_in, y_out, acc_in, acc_out, old_in, old_out,
            send_in, send_out, recv_in, recv_out, x_v, tgt_v, gp, act, unit_in, tmp, dz,
-           recv_sem, send_sem, load_sem, store_sem):
+           recv_sem, send_sem, load_sem, weight_sem):
     n_x, n_y, layers, d, ff, steps, rows = dims
     rb_rows = rows // BLOCKS
     ix, iy = lax.axis_index('tx'), lax.axis_index('ty')
@@ -102,23 +102,34 @@
         return (pltpu.make_async_copy(x_hbm.at[step], x_v, load_sem.at[0]),
                 pltpu.make_async_copy(tgt_hbm.at[step], tgt_v, load_sem.at[1]))
 
-    weight_copies = (pltpu.make_async_copy(win_hbm, p_in, load_sem.at[2]),
-                     pltpu.make_async_copy(wout_hbm, p_out, load_sem.at[3]))
-    for copy in weight_copies + batch_copies(0):
+    def weight_copies(unit):
+        return [pltpu.make_async_copy(src.at[span(side, unit)], dst.at[span(side, unit)], weight_sem.at[side, unit])
+                for side, src, dst in ((0, win_hbm, p_in), (1, wout_hbm, p_out))]
+
+    def first_load(unit, _):
+        for copy in weight_copies(unit):
+            copy.start()
+        return 0
+
+    lax.fori_loop(0, UNITS, first_load, 0)
+    for copy in batch_copies(0):
         copy.start()
-    for copy in weight_copies:
-        copy.wait()
-
-    def first_cast(unit, _):
+
+    def first_cast(unit):
+        for copy in weight_copies(unit):
+            copy.wait()
         for side, weights in ((0, p_in), (1, p_out)):
             at = span(side, unit)
             sends[side][0, at] = weights[at].astype(BF16)
-        return 0
-
-    lax.fori_loop(0, UNITS, first_cast, 0)
+
+    first_cast(0)
     pl.semaphore_wait(barrier, 5)
 
     def first_send(unit, _):
+        @pl.when(unit > 0)
+        def _():
+            first_cast(unit)
+
         send_piece(0, unit, 0)
         return 0
 
@@ -175,8 +186,10 @@
         edge = jnp.logical_or(step == 0, step == steps)
 
         def block(rb, _):
-            kind = jnp.where(step == 0, 0, jnp.where(step == steps, 1, rb % 2))
-            unit = jnp.where(edge, rb, rb // 2)
+            pair = jnp.where(step == 0, rb, rb + 1)
+            kind = jnp.where(step == 0, 0, jnp.where(step == steps, 1, pair % 2))
+            unit = jnp.where(edge, pair, pair // 2)
+            more = jnp.logical_or(step < steps, rb < BLOCKS - 1)
             at = pl.ds(pl.multiple_of(rb * rb_rows, rb_rows), rb_rows)
             hidden = [x_v[at].astype(F32)]
             scales = []
@@ -184,11 +197,19 @@
                 nxt, inv_rms = forward_layer(layer, hidden[-1])
                 hidden.append(nxt)
                 scales.append(inv_rms)
-            forward(0, kind, unit, slot)
+
+            @pl.when(more)
+            def _():
+                forward(0, kind, unit, slot)
+
             grad = ((hidden[-1] - tgt_v[at].astype(F32)) * (2.0 / (rows * d))).astype(BF16)
             for layer in reversed(range(layers)):
                 grad = backward_layer(layer, grad, hidden[layer], scales[layer])
-            forward(1, kind, unit, slot)
+
+            @pl.when(more)
+            def _():
+                forward(1, kind, unit, slot)
+
             return 0
 
         lax.fori_loop(0, BLOCKS, block, 0)
@@ -226,7 +247,15 @@
 
                 lax.fori_loop(0, piece[side] // sub, piece_step, 0)
 
+        first_kind = jnp.where(step < steps - 1, 0, 1)
+
         def unit_step(unit, _):
+            ahead = jnp.logical_and(step < steps, unit == UNITS - 1)
+
+            @pl.when(ahead)
+            def _():
+                forward(0, first_kind, 0, 1 - slot)
+
             @pl.when(step < steps)
             def _():
                 settle(0, unit, slot)
@@ -257,9 +286,17 @@
 
             @pl.when(jnp.logical_and(jnp.logical_not(edge), unit < UNITS // 2))
             def _():
-                for kind in (0, 1):
-                    for side in (0, 1):
-                        forward(side, kind, unit + UNITS // 2, slot)
+                for side in (0, 1):
+                    forward(side, 1, unit + UNITS // 2, slot)
+
+            @pl.when(jnp.logical_and(jnp.logical_not(edge), unit < UNITS // 2 - 1))
+            def _():
+                for side in (0, 1):
+                    forward(side, 0, unit + UNITS // 2 + 1, slot)
+
+            @pl.when(ahead)
+            def _():
+                forward(1, first_kind, 0, 1 - slot)
 
             return 0
 
@@ -267,12 +304,6 @@
         return 0
 
     lax.fori_loop(0, steps + 1, phase, 0)
-    stores = [pltpu.make_async_copy(src, dst, store_sem.at[k]) for k, (src, dst) in enumerate(
-        ((p_in, pin_hbm), (p_out, pout_hbm), (y_in, yin_hbm), (y_out, yout_hbm)))]
-    for copy in stores:
-        copy.start()
-    for copy in stores:
-        copy.wait()
 
 
 def solution(mesh):
@@ -287,11 +318,10 @@
         vmem = pltpu.VMEM
         outs = pl.pallas_call(
             functools.partial(kernel, dims),
-            out_shape=[jax.ShapeDtypeStruct(s, F32) for s in (s_in, s_out, s_in, s_out)],
+            out_shape=[vmem(s, F32) for s in (s_in, s_out, s_in, s_out)],
             in_specs=[pl.BlockSpec(memory_space=pl.ANY)] * 4,
-            out_specs=[pl.BlockSpec(memory_space=pl.ANY)] * 4,
+            out_specs=[pl.BlockSpec(memory_space=vmem)] * 4,
             scratch_shapes=[
-                vmem(s_in, F32), vmem(s_out, F32), vmem(s_in, F32), vmem(s_out, F32),
                 vmem(s_in, F32), vmem(s_out, F32), vmem(s_in, BF16), vmem(s_out, BF16),
                 vmem((2,) + s_in, BF16), vmem((2,) + s_out, BF16),
                 vmem((2, 2, 4) + s_in, BF16), vmem((2, 2, 4) + s_out, BF16),
@@ -300,11 +330,11 @@
                 vmem((layers, rb_rows, d), BF16), vmem((rb_rows, ff), F32), vmem((rb_rows, ff), BF16),
                 pltpu.SemaphoreType.DMA((2, 2, 2, UNITS, 4)),
                 pltpu.SemaphoreType.DMA((2, 2, UNITS, 4)),
-                pltpu.SemaphoreType.DMA((4,)),
-                pltpu.SemaphoreType.DMA((4,)),
+                pltpu.SemaphoreType.DMA((2,)),
+                pltpu.SemaphoreType.DMA((2, UNITS)),
             ],
             compiler_params=pltpu.CompilerParams(
-                collective_id=0, has_side_effects=True, vmem_limit_bytes=67043328),
+                collective_id=0, has_side_effects=True, vmem_limit_bytes=VMEM_LIMIT),
         )(w_in.reshape(s_in), w_out.reshape(s_out), inputs[0, 0], targets[0, 0])
         return tuple(o.reshape(w.shape) for o, w in zip(outs, (w_in, w_out, w_in, w_out)))
 

time: 794 us -> 752 us (0.947)
  Pallas kernels: 784 us -> 746 us
    pallas_call x1, Pallas kernels: 784 us -> 746 us  [device_fn(): pl.pallas_call(functools.partial(kernel, dims), out_shape=[vmem(s, F32) f...]
where the time goes in v2:
time: 752 us
  Pallas kernels  746 us (99%)
    pallas_call x1, Pallas kernels, device_fn(): pl.pallas_call(functools.partial(kernel, dims), out_shape=[vmem(s, F32) f...  746 us

profile of v2, /device:TPU:0, one launch (start us, length us, event | category | flops | bytes accessed | tf_op | source)
XLA Modules:
  0.0 751.5 jit_solution(2279537101834093069)
XLA Ops:
  0.6 745.6 %shard_map.75 = (f32[512,1024]{1,0:T(8,128)S(1)}, f32[2048,256]{1,0:T(8,128)S(1)}, f32[512,1024]{1,0:T(8,128)S(1)}, f32[2048,256]{1,0:T(8,128)S(1)}) custom-call(f32[512,1024]{1,0:T(8,128)} %bitcast.14, f32[2048,256]{1,0:T(8,128)} %bitcast.15, bf16[9,2048,256]{2,1,0:T(8,128)(2,1)} %bitcast.12, bf16[9,2048,256]{2,1,0:T(8,128)(2,1)} %bitcast.13), custom_call_target="tpu_custom_call" | custom-call | tf_op jit(solution)/shard_map/pallas_call | solution.py:319
  746.3 1.3 copy.12
  747.6 1.3 copy.13
  748.9 1.3 copy.14
  750.2 1.3 copy.15

commit v3 on v2

--- a/solution.py
+++ b/solution.py
@@ -24,7 +24,7 @@
 
 
 def kernel(dims, win_hbm, wout_hbm, x_hbm, tgt_hbm, p_in, p_out, y_in, y_out, acc_in, acc_out, old_in, old_out,
-           send_in, send_out, recv_in, recv_out, x_v, tgt_v, gp, act, unit_in, tmp, dz,
+           send_in, send_out, recv_in, recv_out, x_v, tgt_v, gp, act, unit_in, dz,
            recv_sem, send_sem, load_sem, weight_sem):
     n_x, n_y, layers, d, ff, steps, rows = dims
     rb_rows = rows // BLOCKS
@@ -115,22 +115,15 @@
     for copy in batch_copies(0):
         copy.start()
 
-    def first_cast(unit):
-        for copy in weight_copies(unit):
-            copy.wait()
+    pl.semaphore_wait(barrier, 5)
+
+    def first_send(unit, _):
         for side, weights in ((0, p_in), (1, p_out)):
+            weight_copies(unit)[side].wait()
             at = span(side, unit)
             sends[side][0, at] = weights[at].astype(BF16)
-
-    first_cast(0)
-    pl.semaphore_wait(barrier, 5)
-
-    def first_send(unit, _):
-        @pl.when(unit > 0)
-        def _():
-            first_cast(unit)
-
-        send_piece(0, unit, 0)
+            for dest in (2, 1, 0):
+                direct(side, 0, unit, 0, dest).start()
         return 0
 
     lax.fori_loop(0, UNITS, first_send, 0)
@@ -141,33 +134,26 @@
         inv_rms = lax.rsqrt(jnp.mean(hidden * hidden, axis=-1, keepdims=True) + EPS)
         normed = (hidden * inv_rms).astype(BF16)
         unit_in[layer] = normed
-        gp[layer] = dot(normed, w_in, 1, 0)
-
-        def activate(i, _):
-            at = pl.ds(pl.multiple_of(i * 16, 16), 16)
-            z = gp[layer, at]
+        cols = ff // 4
+        for f in range(4):
+            at = slice(f * cols, (f + 1) * cols)
+            z = dot(normed, w_in[:, at], 1, 0)
             z2 = z * z
             tanh = jnp.tanh(z * (GELU_C0 + GELU_C1 * z2))
             cdf = 0.5 + 0.5 * tanh
-            act[layer, at] = (z * cdf).astype(BF16)
-            gp[layer, at] = cdf + (0.5 * z * (1.0 - tanh * tanh)) * (GELU_C0 + (3.0 * GELU_C1) * z2)
-            return 0
-
-        lax.fori_loop(0, rb_rows // 16, activate, 0)
+            act[layer, :, at] = (z * cdf).astype(BF16)
+            gp[layer, :, at] = cdf + (0.5 * z * (1.0 - tanh * tanh)) * (GELU_C0 + (3.0 * GELU_C1) * z2)
         out = dot(act[layer], w_out, 1, 0)
         return (hidden + out).astype(BF16).astype(F32), inv_rms
 
     def backward_layer(layer, grad_b, hidden, inv_rms):
         w_in = send_in[0, layer * d:(layer + 1) * d]
         w_out = send_out[0, layer * ff:(layer + 1) * ff]
-        tmp[...] = dot(grad_b, w_out, 1, 1)
-
-        def chain(i, _):
-            at = pl.ds(pl.multiple_of(i * 16, 16), 16)
-            dz[at] = (tmp[at].astype(BF16).astype(F32) * gp[layer, at]).astype(BF16)
-            return 0
-
-        lax.fori_loop(0, rb_rows // 16, chain, 0)
+        rows_f = ff // 4
+        for f in range(4):
+            at = slice(f * rows_f, (f + 1) * rows_f)
+            da = dot(grad_b, w_out[at], 1, 1).astype(BF16).astype(F32)
+            dz[:, at] = (da * gp[layer, :, at]).astype(BF16)
         acc_out[layer * ff:(layer + 1) * ff] += dot(act[layer], grad_b, 0, 0)
         acc_in[layer * d:(layer + 1) * d] += dot(unit_in[layer], dz[...], 0, 0)
         if layer == 0:
@@ -186,10 +172,12 @@
         edge = jnp.logical_or(step == 0, step == steps)
 
         def block(rb, _):
-            pair = jnp.where(step == 0, rb, rb + 1)
+            pair = jnp.where(step == 0, rb, jnp.where(step == steps, jnp.minimum(rb + 1, BLOCKS - 1), rb + 1))
             kind = jnp.where(step == 0, 0, jnp.where(step == steps, 1, pair % 2))
             unit = jnp.where(edge, pair, pair // 2)
-            more = jnp.logical_or(step < steps, rb < BLOCKS - 1)
+            late = jnp.logical_and(step == steps, rb >= BLOCKS - 2)
+            early = jnp.logical_and(step == 0, rb == BLOCKS - 1)
+            last = rb == BLOCKS - 1
             at = pl.ds(pl.multiple_of(rb * rb_rows, rb_rows), rb_rows)
             hidden = [x_v[at].astype(F32)]
             scales = []
@@ -198,17 +186,25 @@
                 hidden.append(nxt)
                 scales.append(inv_rms)
 
-            @pl.when(more)
+            @pl.when(jnp.logical_not(jnp.logical_and(edge, last)))
             def _():
                 forward(0, kind, unit, slot)
+
+            @pl.when(jnp.logical_and(late, last))
+            def _():
+                forward(1, kind, unit, slot)
 
             grad = ((hidden[-1] - tgt_v[at].astype(F32)) * (2.0 / (rows * d))).astype(BF16)
             for layer in reversed(range(layers)):
                 grad = backward_layer(layer, grad, hidden[layer], scales[layer])
 
-            @pl.when(more)
+            @pl.when(jnp.logical_not(jnp.logical_or(late, early)))
             def _():
                 forward(1, kind, unit, slot)
+
+            @pl.when(early)
+            def _():
+                forward(0, kind, unit, slot)
 
             return 0
 
@@ -283,6 +279,10 @@
             @pl.when(step < steps)
             def _():
                 send_piece(1, unit, 1 - slot)
+
+            @pl.when(jnp.logical_and(step == 0, unit == 0))
+            def _():
+                forward(1, 0, UNITS - 1, slot)
 
             @pl.when(jnp.logical_and(jnp.logical_not(edge), unit < UNITS // 2))
             def _():
@@ -327,7 +327,7 @@
                 vmem((2, 2, 4) + s_in, BF16), vmem((2, 2, 4) + s_out, BF16),
                 vmem((rows, d), BF16), vmem((rows, d), BF16),
                 vmem((layers, rb_rows, ff), F32), vmem((layers, rb_rows, ff), BF16),
-                vmem((layers, rb_rows, d), BF16), vmem((rb_rows, ff), F32), vmem((rb_rows, ff), BF16),
+                vmem((layers, rb_rows, d), BF16), vmem((rb_rows, ff), BF16),
                 pltpu.SemaphoreType.DMA((2, 2, 2, UNITS, 4)),
                 pltpu.SemaphoreType.DMA((2, 2, UNITS, 4)),
                 pltpu.SemaphoreType.DMA((2,)),

time: 752 us -> 744 us (0.989)
  Pallas kernels: 746 us -> 738 us
    pallas_call x1, Pallas kernels: 746 us -> 738 us  [device_fn(): pl.pallas_call(functools.partial(kernel, dims), out_shape=[vmem(s, F32) f...]
where the time goes in v3:
time: 744 us
  Pallas kernels  738 us (99%)
    pallas_call x1, Pallas kernels, device_fn(): pl.pallas_call(functools.partial(kernel, dims), out_shape=[vmem(s, F32) f...  738 us

profile of v3, /device:TPU:0, one launch (start us, length us, event | category | flops | bytes accessed | tf_op | source)
XLA Modules:
  0.0 743.6 jit_solution(2637447856062204470)
XLA Ops:
  0.6 737.7 %shard_map.75 = (f32[512,1024]{1,0:T(8,128)S(1)}, f32[2048,256]{1,0:T(8,128)S(1)}, f32[512,1024]{1,0:T(8,128)S(1)}, f32[2048,256]{1,0:T(8,128)S(1)}) custom-call(f32[512,1024]{1,0:T(8,128)} %bitcast.14, f32[2048,256]{1,0:T(8,128)} %bitcast.15, bf16[9,2048,256]{2,1,0:T(8,128)(2,1)} %bitcast.12, bf16[9,2048,256]{2,1,0:T(8,128)(2,1)} %bitcast.13), custom_call_target="tpu_custom_call" | custom-call | tf_op jit(solution)/shard_map/pallas_call | solution.py:319
  738.3 1.3 copy.12
  739.6 1.3 copy.13
  740.9 1.3 copy.14
  742.3 1.3 copy.15

commit v4 on v3

--- a/solution.py
+++ b/solution.py
@@ -12,6 +12,7 @@
 VMEM_LIMIT = 54 * 1024 * 1024
 UNITS = 8
 BLOCKS = 8
+RELAYED = 5
 GELU_C0 = 0.7978845608028654
 GELU_C1 = 0.044715 * GELU_C0
 F32 = jnp.float32
@@ -42,10 +43,6 @@
     y_dir = 3 - py
     z_dir = 2 + py
 
-    barrier = pltpu.get_barrier_semaphore()
-    for peer in (to_partner, to_opposite, to_y, to_z, {'tx': ix, 'ty': relay_from}):
-        pl.semaphore_signal(barrier, inc=1, device_id=peer, device_id_type=MESH)
-
     piece = ((layers * d) // UNITS, (layers * ff) // UNITS)
     sends = (send_in, send_out)
     recvs = (recv_in, recv_out)
@@ -106,27 +103,38 @@
         return [pltpu.make_async_copy(src.at[span(side, unit)], dst.at[span(side, unit)], weight_sem.at[side, unit])
                 for side, src, dst in ((0, win_hbm, p_in), (1, wout_hbm, p_out))]
 
+    for copy in weight_copies(0):
+        copy.start()
+    barrier = pltpu.get_barrier_semaphore()
+    for peer in (to_partner, to_opposite, to_y, to_z, {'tx': ix, 'ty': relay_from}):
+        pl.semaphore_signal(barrier, inc=1, device_id=peer, device_id_type=MESH)
+
+    def first_piece(unit, wait):
+        for side, weights in ((0, p_in), (1, p_out)):
+            weight_copies(unit)[side].wait()
+            at = span(side, unit)
+            sends[side][0, at] = weights[at].astype(BF16)
+            if wait and side == 0:
+                pl.semaphore_wait(barrier, 5)
+            for dest in (2, 1, 0):
+                direct(side, 0, unit, 0, dest).start()
+
+    first_piece(0, True)
+
     def first_load(unit, _):
         for copy in weight_copies(unit):
             copy.start()
         return 0
 
-    lax.fori_loop(0, UNITS, first_load, 0)
+    lax.fori_loop(1, UNITS, first_load, 0)
     for copy in batch_copies(0):
         copy.start()
 
-    pl.semaphore_wait(barrier, 5)
-
     def first_send(unit, _):
-        for side, weights in ((0, p_in), (1, p_out)):
-            weight_copies(unit)[side].wait()
-            at = span(side, unit)
-            sends[side][0, at] = weights[at].astype(BF16)
-            for dest in (2, 1, 0):
-                direct(side, 0, unit, 0, dest).start()
+        first_piece(unit, False)
         return 0
 
-    lax.fori_loop(0, UNITS, first_send, 0)
+    lax.fori_loop(1, UNITS, first_send, 0)
 
     def forward_layer(layer, hidden):
         w_in = send_in[0, layer * d:(layer + 1) * d]
@@ -172,7 +180,7 @@
         edge = jnp.logical_or(step == 0, step == steps)
 
         def block(rb, _):
-            pair = jnp.where(step == 0, rb, jnp.where(step == steps, jnp.minimum(rb + 1, BLOCKS - 1), rb + 1))
+            pair = jnp.where(step == 0, rb, jnp.where(step == steps, jnp.minimum(rb + 1, BLOCKS - 1), rb + 2))
             kind = jnp.where(step == 0, 0, jnp.where(step == steps, 1, pair % 2))
             unit = jnp.where(edge, pair, pair // 2)
             late = jnp.logical_and(step == steps, rb >= BLOCKS - 2)
@@ -250,7 +258,13 @@
 
             @pl.when(ahead)
             def _():
-                forward(0, first_kind, 0, 1 - slot)
+                for side in (0, 1):
+                    forward(side, first_kind, 0, 1 - slot)
+
+            @pl.when(jnp.logical_and(ahead, step < steps - 1))
+            def _():
+                for side in (0, 1):
+                    forward(side, 1, 0, 1 - slot)
 
             @pl.when(step < steps)
             def _():
@@ -284,19 +298,11 @@
             def _():
                 forward(1, 0, UNITS - 1, slot)
 
-            @pl.when(jnp.logical_and(jnp.logical_not(edge), unit < UNITS // 2))
-            def _():
-                for side in (0, 1):
-                    forward(side, 1, unit + UNITS // 2, slot)
-
-            @pl.when(jnp.logical_and(jnp.logical_not(edge), unit < UNITS // 2 - 1))
-            def _():
-                for side in (0, 1):
-                    forward(side, 0, unit + UNITS // 2 + 1, slot)
-
-            @pl.when(ahead)
-            def _():
-                forward(1, first_kind, 0, 1 - slot)
+            @pl.when(jnp.logical_and(jnp.logical_not(edge), unit < UNITS - RELAYED))
+            def _():
+                for kind in (0, 1):
+                    for side in (0, 1):
+                        forward(side, kind, unit + RELAYED, slot)
 
             return 0
 

time: 744 us -> 744 us (level)
  no operation moved by 1% of the time
where the time goes in v4:
time: 744 us
  Pallas kernels  738 us (99%)
    pallas_call x1, Pallas kernels, device_fn(): pl.pallas_call(functools.partial(kernel, dims), out_shape=[vmem(s, F32) f...  738 us

profile of v4, /device:TPU:0, one launch (start us, length us, event | category | flops | bytes accessed | tf_op | source)
XLA Modules:
  0.0 743.5 jit_solution(1100896528133554226)
XLA Ops:
  0.6 737.6 %shard_map.75 = (f32[512,1024]{1,0:T(8,128)S(1)}, f32[2048,256]{1,0:T(8,128)S(1)}, f32[512,1024]{1,0:T(8,128)S(1)}, f32[2048,256]{1,0:T(8,128)S(1)}) custom-call(f32[512,1024]{1,0:T(8,128)} %bitcast.14, f32[2048,256]{1,0:T(8,128)} %bitcast.15, bf16[9,2048,256]{2,1,0:T(8,128)(2,1)} %bitcast.12, bf16[9,2048,256]{2,1,0:T(8,128)(2,1)} %bitcast.13), custom_call_target="tpu_custom_call" | custom-call | tf_op jit(solution)/shard_map/pallas_call | solution.py:325
  738.2 1.3 copy.12
  739.5 1.3 copy.13
  740.9 1.3 copy.14
  742.2 1.3 copy.15

commit v5 on v4

--- a/solution.py
+++ b/solution.py
@@ -310,6 +310,20 @@
         return 0
 
     lax.fori_loop(0, steps + 1, phase, 0)
+
+
+def store_kernel(*refs):
+    count = len(refs) // 2
+    copies = []
+    for k in range(count):
+        half = refs[k].shape[0] // 2
+        for part in range(2):
+            at = pl.ds(part * half, half)
+            copies.append(pltpu.make_async_copy(refs[k].at[at], refs[count + k].at[at], refs[-1].at[k, part]))
+    for copy in copies:
+        copy.start()
+    for copy in copies:
+        copy.wait()
 
 
 def solution(mesh):
@@ -342,6 +356,14 @@
             compiler_params=pltpu.CompilerParams(
                 collective_id=0, has_side_effects=True, vmem_limit_bytes=VMEM_LIMIT),
         )(w_in.reshape(s_in), w_out.reshape(s_out), inputs[0, 0], targets[0, 0])
+        outs = pl.pallas_call(
+            store_kernel,
+            out_shape=[jax.ShapeDtypeStruct(s, F32) for s in (s_in, s_out, s_in, s_out)],
+            in_specs=[pl.BlockSpec(memory_space=pl.ANY)] * 4,
+            out_specs=[pl.BlockSpec(memory_space=pl.ANY)] * 4,
+            scratch_shapes=[pltpu.SemaphoreType.DMA((4, 2))],
+            compiler_params=pltpu.CompilerParams(vmem_limit_bytes=2 * 1024 * 1024),
+        )(*outs)
         return tuple(o.reshape(w.shape) for o, w in zip(outs, (w_in, w_out, w_in, w_out)))
 
     block_spec = P('tx', 'ty')

time: 744 us -> 742 us (level)
  no operation moved by 1% of the time
where the time goes in v5:
time: 742 us
  Pallas kernels  741 us (100%)
    pallas_call x1, Pallas kernels, device_fn(): pl.pallas_call(functools.partial(kernel, dims), out_shape=[vmem(s, F32) f...  738 us

profile of v5, /device:TPU:0, one launch (start us, length us, event | category | flops | bytes accessed | tf_op | source)
XLA Modules:
  0.0 741.6 jit_solution(3008951036685212344)
XLA Ops:
  0.6 737.6 %shard_map.75 = (f32[512,1024]{1,0:T(8,128)S(1)}, f32[2048,256]{1,0:T(8,128)S(1)}, f32[512,1024]{1,0:T(8,128)S(1)}, f32[2048,256]{1,0:T(8,128)S(1)}) custom-call(f32[512,1024]{1,0:T(8,128)} %bitcast.10, f32[2048,256]{1,0:T(8,128)} %bitcast.11, bf16[9,2048,256]{2,1,0:T(8,128)(2,1)} %bitcast.8, bf16[9,2048,256]{2,1,0:T(8,128)(2,1)} %bitcast.9), custom_call_target="tpu_custom_call" | custom-call | tf_op jit(solution)/shard_map/pallas_call | solution.py:339
  738.2 3.4 shard_map.76
